TPU v7x, 32 devices: a whole 2x2x4 slice. The times are simulated.
32 devices in a mesh: texel: 8 (over y, x, core), light: 4 (over z).
Axes of the slice: x: 2, y: 2, z: 4, core: 2. Of those that a mesh axis runs over, the one named last changes fastest.
Arguments:
- tex_feat: bfloat16 [8192, 512], P('texel'), may hold values from -18 to 18
- light_feat: bfloat16 [6144, 512], P('light'), may hold values from -0.25 to 0.25
- sketch: bfloat16 [6144, 256], P('light'), may hold values from -0.078125 to 0.078125
- row_counts: int32 [8], replicated, may hold values from 1 to 1024, 4096 in all
Outputs:
- basis: float32 [8192, 256], P('texel')
- coeffs: float32 [256, 6144], P('texel', 'light')
Inputs may be any that keep to these rules, and one draw needn't show every extreme that they name: row_counts sums to 8 * 512; some entry equals 1024.
All inputs are finite; a program needn't handle non-finite values.
Results may differ from a plain program's by a relative error of at most 0.0034.
Values sent between devices are 32-bit elements; how exact they have to be, the bound alone decides.
A program may use at most 64 MiB of HBM per device.

v0:
```python
import jax
import jax.numpy as jnp
from jax import lax
from jax.sharding import PartitionSpec as P


def on_device(tex_feat, light_feat, sketch, row_counts):
    capacity = tex_feat.shape[0]
    own_count = row_counts[lax.axis_index("texel")]
    valid_total = jnp.sum(row_counts).astype(jnp.float32)
    logits = lax.dot_general(
        tex_feat, light_feat, (((1,), (1,)), ((), ())), preferred_element_type=jnp.float32
    )
    tile_block = jnp.sin(logits).astype(jnp.bfloat16)
    row_valid = (lax.iota(jnp.int32, capacity) < own_count).astype(jnp.float32)
    partial_value = (
        jnp.dot(tile_block, sketch, preferred_element_type=jnp.float32) * row_valid[:, None]
    )
    sketched = lax.psum(partial_value, "light")
    gram_local = jnp.dot(sketched.T, sketched, precision=lax.Precision.HIGHEST)
    gram_matrix = lax.psum(gram_local, "texel") / valid_total
    factor = jnp.linalg.cholesky(gram_matrix)
    basis = jax.scipy.linalg.solve_triangular(factor, sketched.T, lower=True).T
    basis_half = basis.astype(jnp.bfloat16)
    coeffs = lax.psum_scatter(
        lax.dot_general(
            basis_half, tile_block, (((0,), (0,)), ((), ())), preferred_element_type=jnp.float32
        ),
        "texel",
        scatter_dimension=0,
        tiled=True,
    ) / jnp.sqrt(valid_total)
    return (basis, coeffs)


def solution(mesh):
    placed = (P("texel", None), P("light", None), P("light", None), P())
    return jax.shard_map(
        on_device,
        mesh=mesh,
        in_specs=placed,
        out_specs=(P("texel", None), P("texel", "light")),
        check_vma=False,
    )
```

profile of v0, /device:TPU:0, one launch (start us, length us, event | category | flops | bytes accessed | tf_op | source)
XLA Modules:
  0.0 261.9 jit_solution(2642677506085759507)
XLA Ops:
  7.2 1.3 dynamic_slice.3
  8.6 0.6 fusion.10
  9.3 23.0 %sine_convert_fusion = bf16[1024,1536]{1,0:T(8,128)(2,1)S(1)} fusion(bf16[1024,512]{1,0:T(8,128)(2,1)} %param.4, bf16[1536,512]{1,0:T(8,128)(2,1)S(1)} %copy-done), kind=kOutput, calls=%fused_computation.2 | convolution fusion | flops 1612185600 | bytes 5767168 | tf_op jit(solution)/shard_map/dot_general | solution.py:11
  32.2 1.7 copy-done.2
  33.9 1.9 convolution_multiply_fusion
  35.9 54.7 %all-reduce.4.cloned.1.call-done = f32[1024,256]{1,0:T(8,128)} async-done(((f32[1024,256]{1,0:T(8,128)}), f32[1024,256]{1,0:T(8,128)}) %all-reduce.4.cloned.1.call-update) | async-done | bytes 1048592 | tf_op jit(solution)/shard_map/psum | solution.py:19
  90.6 4.1 %fusion.12 = f32[256,256]{0,1:T(8,128)} fusion(f32[1024,256]{1,0:T(8,128)} %all-reduce.4.cloned.1.call-done), kind=kOutput, calls=%fused_computation.37 | convolution fusion | flops 805306368 | bytes 1310720 | tf_op jit(solution)/shard_map/dot_general | solution.py:20
  94.8 0.2 reduce-scatter.2.cloned.1.call-start
  95.1 0.6 reduce_sum.9
  96.3 51.8 %all-reduce.6.cloned.1.call-done = f32[256,256]{0,1:T(8,128)} async-done(((f32[256,256]{0,1:T(8,128)}), f32[256,256]{0,1:T(8,128)}) %all-reduce.6.cloned.1.call-update) | async-done | bytes 262160 | tf_op jit(solution)/shard_map/psum | solution.py:21
  148.1 1.0 broadcast_divide_fusion
  149.2 1.0 fusion.4
  150.2 11.7 %cholesky.50 = f32[128,128]{1,0:T(8,128)S(1)} custom-call(f32[128,128]{1,0:T(8,128)S(1)} %cholesky.118), custom_call_target="Cholesky" | custom-call | tf_op jit(solution)/shard_map/jit(cholesky)/cholesky | solution.py:22
  162.0 9.8 %custom-call.15 = f32[1,128,128]{1,2,0:T(8,128)S(1)} custom-call(f32[1,128,128]{2,1,0:T(8,128)S(1)} %get-tuple-element.25), custom_call_target="InvertDiagBlocksLowerTriangular" | custom-call | tf_op jit(solution)/shard_map/jit(cholesky)/cholesky | solution.py:22
  172.0 0.3 convolution_subtract_fusion.1
  172.3 11.7 %cholesky.105 = f32[128,128]{1,0:T(8,128)S(1)} custom-call(f32[128,128]{1,0:T(8,128)S(1)} %convolution_subtract_fusion.1), custom_call_target="Cholesky" | custom-call | tf_op jit(solution)/shard_map/jit(cholesky)/cholesky | solution.py:22
  184.1 0.7 compare_reduce_fusion
  186.1 4.1 %while.1 = (s32[]{:T(128)}, f32[256,256]{1,0:T(8,128)S(1)}, s32[2,2]{1,0:T(2,128)S(1)}, f32[2,128,128]{2,1,0:T(8,128)S(1)}, s32[]{:T(128)}) while((s32[]{:T(128)}, f32[256,256]{1,0:T(8,128)S(1)}, s32[2,2]{1,0:T(2,128)S(1)}, f32[2,128,128]{2,1,0:T(8,128)S(1)}, s32[]{:T(128)}) %tuple.28), condition=%wide.while_cond, body=%wide.while_body.sunk | while | flops 2 | bytes 131189 | solution.py:23
  186.3 0.6 fusion.25
  186.9 1.4 bitcast_dynamic-update-slice_fusion.2
  188.3 0.6 fusion.25
  188.8 1.4 bitcast_dynamic-update-slice_fusion.2
  190.2 0.6 copy-done.5
  190.9 20.5 %custom-call.16 = f32[2,128,128]{1,2,0:T(8,128)S(1)} custom-call(f32[2,128,128]{2,1,0:T(8,128)} %copy-done.5), custom_call_target="InvertDiagBlocksLowerTriangular" | custom-call | tf_op jit(solution)/shard_map/jit(_solve_triangular)/triangular_solve | solution.py:23
  211.4 0.6 fusion
  212.0 1.0 convolution_subtract_fusion
  213.0 0.6 fusion.6
  213.7 2.2 fusion.2
  215.9 1.1 maximum_bitcast_fusion
  217.0 2.5 copy.8
  219.5 34.2 %reduce-scatter.2.cloned.1.call-done = f32[32,1536]{1,0:T(8,128)} async-done(((f32[256,1536]{1,0:T(8,128)}), f32[32,1536]{1,0:T(8,128)}) %reduce-scatter.2.cloned.1.call-update) | async-done | bytes 196624 | tf_op jit(solution)/shard_map/reduce_scatter | solution.py:25
  253.7 1.6 broadcast_divide_fusion.1
  (29 shorter events, 0.7 us)
Async XLA Ops:
  7.2 2.1 copy-start
  7.2 83.5 %all-reduce.4.cloned.1.call-start = ((), (), s32[]{:S(2)}) async-start(), calls=%async_computation.1 | async-start | bytes 2097152 | tf_op jit(solution)/shard_map/psum | solution.py:19
  9.2 24.7 %copy-start.4 = (bf16[1536,256]{1,0:T(8,128)(2,1)S(1)}, bf16[1536,256]{1,0:T(8,128)(2,1)}, u32[]{:S(2)}) copy-start(bf16[1536,256]{1,0:T(8,128)(2,1)} %param.6) | copy-start | bytes 2359300
  32.2 1.7 copy-start.2
  35.8 59.2 %copy-start.6 = (s32[8]{0:T(128)S(1)}, s32[8]{0:T(128)}, u32[]{:S(2)}) copy-start(s32[8]{0:T(128)} %param.7) | copy-start | bytes 100
  35.9 112.3 %all-reduce.6.cloned.1.call-start = ((), (), s32[]{:S(2)}) async-start(), calls=%async_computation.2 | async-start | bytes 524288 | tf_op jit(solution)/shard_map/psum | solution.py:21
  90.6 120.7 %copy-start.1 = (f32[1024,256]{1,0:T(8,128)S(1)}, f32[1024,256]{1,0:T(8,128)}, u32[]{:S(2)}) copy-start(f32[1024,256]{1,0:T(8,128)} %all-reduce.4.cloned.1.call-done) | copy-start | bytes 3145732
  94.8 158.9 %reduce-scatter.2.cloned.1.call-start = ((), (), s32[]{:S(2)}) async-start(), calls=%async_computation.3 | async-start | bytes 1769472 | tf_op jit(solution)/shard_map/reduce_scatter | solution.py:25
  190.2 0.7 copy-start.5
  211.4 2.3 copy-start.3
Sparse Core Ops, SparseCore 0:
  36.0 54.6 all-reduce.3
  94.9 53.1 all-reduce.5
  216.0 37.6 reduce-scatter.1
where the time goes:
time: 262 us
  waiting for transfers between devices  141 us (54%)
  other arithmetic  60.4 us (23%)
  matrix products  34 us (13%)
  between operations  15.8 us (6%)
  local copies, waits for them, and re-layouts  10.3 us (4%)
    psum x1, waiting for transfers between devices, on_device(): sketched = lax.psum(partial_value, 'light')  54.7 us
    psum x1, waiting for transfers between devices, on_device(): gram_matrix = lax.psum(gram_local, 'texel') / valid_total  51.8 us
    reduce_scatter x1, waiting for transfers between devices, on_device(): lax.psum_scatter(lax.dot_general(basis_half, tile_block, (((0,), (0,)), (...  34.2 us
    another operation x6, other arithmetic, on_device(): factor = jnp.linalg.cholesky(gram_matrix)  34 us
    dot_general x1, matrix products, on_device(): lax.dot_general(tex_feat, light_feat, (((1,), (1,)), ((), ())), preferred...  23 us
    another operation x3, other arithmetic, on_device(): basis = jax.scipy.linalg.solve_triangular(factor, sketched.T, lower=True).T  20.5 us
  transfers between devices with their start and end apart: 3, of which 3 were waited for; matrix products, arithmetic and copies ran while one was open for 2% of the time, Pallas kernels for 0%

commit v1 on v0

--- a/solution.py
+++ b/solution.py
@@ -16,7 +16,11 @@
     partial_value = (
         jnp.dot(tile_block, sketch, preferred_element_type=jnp.float32) * row_valid[:, None]
     )
-    sketched = lax.psum(partial_value, "light")
+    sketched = partial_value
+    for hop in (1, 2):
+        sketched = sketched + lax.ppermute(
+            sketched, "light", [(dev, dev ^ hop) for dev in range(4)]
+        )
     gram_local = jnp.dot(sketched.T, sketched, precision=lax.Precision.HIGHEST)
     gram_matrix = lax.psum(gram_local, "texel") / valid_total
     factor = jnp.linalg.cholesky(gram_matrix)

time: 262 us -> 283 us (1.080)
  waiting for transfers between devices: 141 us -> 154 us
  starting transfers between devices: 0.3 us -> 6.18 us
    ppermute x0 -> x2, waiting for transfers between devices: none -> 66.8 us  [on_device(): lax.ppermute(sketched, 'light', [(dev, dev ^ hop) for dev in range(4)])]
    psum x1 -> x0, waiting for transfers between devices: 54.7 us -> none  [on_device(): sketched = lax.psum(partial_value, 'light')]
    ppermute x0 -> x2, starting transfers between devices: none -> 5.92 us  [on_device(): lax.ppermute(sketched, 'light', [(dev, dev ^ hop) for dev in range(4)])]
  transfers between devices with their start and end apart: 3 -> 4, of which waited for: 3 -> 4; matrix products, arithmetic and copies ran while one was open for 2% -> 2% of each run, Pallas kernels for 0% -> 0%
where the time goes in v1:
time: 283 us
  waiting for transfers between devices  154 us (54%)
  other arithmetic  62.9 us (22%)
  matrix products  34 us (12%)
  between operations  16.3 us (6%)
  local copies, waits for them, and re-layouts  9.45 us (3%)
  starting transfers between devices  6.18 us (2%)
    ppermute x2, waiting for transfers between devices, on_device(): lax.ppermute(sketched, 'light', [(dev, dev ^ hop) for dev in range(4)])  66.8 us
    psum x1, waiting for transfers between devices, on_device(): gram_matrix = lax.psum(gram_local, 'texel') / valid_total  52.5 us
    reduce_scatter x1, waiting for transfers between devices, on_device(): lax.psum_scatter(lax.dot_general(basis_half, tile_block, (((0,), (0,)), (...  34.2 us
    another operation x6, other arithmetic, on_device(): factor = jnp.linalg.cholesky(gram_matrix)  34 us
    dot_general x1, matrix products, on_device(): lax.dot_general(tex_feat, light_feat, (((1,), (1,)), ((), ())), preferred...  23 us
    another operation x3, other arithmetic, on_device(): basis = jax.scipy.linalg.solve_triangular(factor, sketched.T, lower=True).T  20.5 us
    ppermute x2, starting transfers between devices, on_device(): lax.ppermute(sketched, 'light', [(dev, dev ^ hop) for dev in range(4)])  5.92 us
  transfers between devices with their start and end apart: 4, of which 4 were waited for; matrix products, arithmetic and copies ran while one was open for 2% of the time, Pallas kernels for 0%

profile of v1, /device:TPU:0, one launch (start us, length us, event | category | flops | bytes accessed | tf_op | source)
XLA Modules:
  0.0 282.6 jit_solution(2622502421054951745)
XLA Ops:
  7.2 1.3 dynamic_slice.3
  8.6 0.6 fusion.13
  9.3 23.0 %sine_convert_fusion = bf16[1024,1536]{1,0:T(8,128)(2,1)S(1)} fusion(bf16[1024,512]{1,0:T(8,128)(2,1)} %param.4, bf16[1536,512]{1,0:T(8,128)(2,1)S(1)} %copy-done), kind=kOutput, calls=%fused_computation.2 | convolution fusion | flops 1612185600 | bytes 5767168 | tf_op jit(solution)/shard_map/dot_general | solution.py:11
  32.2 1.0 convolution_multiply_fusion
  33.2 0.7 copy-done.2
  33.9 3.1 %collective-permute-start = (f32[1024,256]{1,0:T(8,128)S(1)}, f32[1024,256]{1,0:T(8,128)S(1)}, u32[]{:S(2)}, u32[]{:S(2)}) collective-permute-start(f32[1024,256]{1,0:T(8,128)S(1)} %convolution_multiply_fusion), channel_id=1, source_target_pairs={{0,1},{1,0},{2,3},{3,2},{4,5},{5,4},{6,7},{7,6},{8,9},{9,8},{10,11... | collective-permute-start | bytes 3145736 | tf_op jit(solution)/shard_map/ppermute | solution.py:21
  37.0 23.1 %collective-permute-done = f32[1024,256]{1,0:T(8,128)S(1)} collective-permute-done((f32[1024,256]{1,0:T(8,128)S(1)}, f32[1024,256]{1,0:T(8,128)S(1)}, u32[]{:S(2)}, u32[]{:S(2)}) %collective-permute-start) | collective-permute-done | bytes 1048608 | tf_op jit(solution)/shard_map/ppermute | solution.py:21
  60.2 2.8 %collective-permute-start.1 = (f32[1024,256]{1,0:T(8,128)S(1)}, f32[1024,256]{1,0:T(8,128)}, u32[]{:S(2)}, u32[]{:S(2)}) collective-permute-start(f32[1024,256]{1,0:T(8,128)S(1)} %add.37), channel_id=1, source_target_pairs={{0,2},{1,3},{2,0},{3,1},{4,6},{5,7},{6,4},{7,5},{8,10},{9,11},{10,... | collective-permute-start | bytes 3145736 | tf_op jit(solution)/shard_map/ppermute | solution.py:21
  63.1 0.6 reduce_sum.9
  64.4 43.7 %collective-permute-done.1 = f32[1024,256]{1,0:T(8,128)} collective-permute-done((f32[1024,256]{1,0:T(8,128)S(1)}, f32[1024,256]{1,0:T(8,128)}, u32[]{:S(2)}, u32[]{:S(2)}) %collective-permute-start.1) | collective-permute-done | bytes 1048608 | tf_op jit(solution)/shard_map/ppermute | solution.py:21
  108.1 4.1 %fusion.5 = f32[256,256]{0,1:T(8,128)} fusion(f32[1024,256]{1,0:T(8,128)S(1)} %add.37, f32[1024,256]{1,0:T(8,128)} %collective-permute-done.1), kind=kOutput, calls=%fused_computation.13 | convolution fusion | flops 805568512 | bytes 2359296 | tf_op jit(solution)/shard_map/dot_general | solution.py:24
  112.4 2.3 add_bitcast_fusion
  114.7 52.5 %all-reduce.3.cloned.1.call-done = f32[256,256]{0,1:T(8,128)} async-done(((f32[256,256]{0,1:T(8,128)}), f32[256,256]{0,1:T(8,128)}) %all-reduce.3.cloned.1.call-update) | async-done | bytes 262160 | tf_op jit(solution)/shard_map/psum | solution.py:25
  167.2 1.0 broadcast_divide_fusion
  168.3 1.0 fusion.7
  169.4 11.7 %cholesky.50 = f32[128,128]{1,0:T(8,128)S(1)} custom-call(f32[128,128]{1,0:T(8,128)S(1)} %cholesky.118), custom_call_target="Cholesky" | custom-call | tf_op jit(solution)/shard_map/jit(cholesky)/cholesky | solution.py:26
  181.1 9.8 %custom-call.15 = f32[1,128,128]{1,2,0:T(8,128)S(1)} custom-call(f32[1,128,128]{2,1,0:T(8,128)S(1)} %get-tuple-element.25), custom_call_target="InvertDiagBlocksLowerTriangular" | custom-call | tf_op jit(solution)/shard_map/jit(cholesky)/cholesky | solution.py:26
  191.4 11.7 %cholesky.105 = f32[128,128]{1,0:T(8,128)S(1)} custom-call(f32[128,128]{1,0:T(8,128)S(1)} %convolution_subtract_fusion), custom_call_target="Cholesky" | custom-call | tf_op jit(solution)/shard_map/jit(cholesky)/cholesky | solution.py:26
  203.2 0.7 compare_reduce_fusion
  205.3 4.2 %while.1 = (s32[]{:T(128)}, f32[256,256]{1,0:T(8,128)S(1)}, s32[2,2]{1,0:T(2,128)S(1)}, f32[2,128,128]{2,1,0:T(8,128)S(1)}, s32[]{:T(128)}) while((s32[]{:T(128)}, f32[256,256]{1,0:T(8,128)S(1)}, s32[2,2]{1,0:T(2,128)S(1)}, f32[2,128,128]{2,1,0:T(8,128)S(1)}, s32[]{:T(128)}) %tuple.28), condition=%wide.while_cond, body=%wide.while_body.sunk | while | flops 2 | bytes 131189 | solution.py:27
  206.1 1.4 bitcast_dynamic-update-slice_fusion.2
  208.1 1.4 bitcast_dynamic-update-slice_fusion.2
  209.6 0.6 copy-done.5
  210.2 20.5 %custom-call.16 = f32[2,128,128]{1,2,0:T(8,128)S(1)} custom-call(f32[2,128,128]{2,1,0:T(8,128)} %copy-done.5), custom_call_target="InvertDiagBlocksLowerTriangular" | custom-call | tf_op jit(solution)/shard_map/jit(_solve_triangular)/triangular_solve | solution.py:27
  230.7 0.6 fusion.1
  231.4 1.0 fusion.8
  232.4 1.7 fusion
  234.1 2.2 fusion.3
  236.3 1.0 maximum_bitcast_fusion
  237.4 2.5 copy.8
  239.9 34.2 %reduce-scatter.2.cloned.1.call-done = f32[32,1536]{1,0:T(8,128)} async-done(((f32[256,1536]{1,0:T(8,128)}), f32[32,1536]{1,0:T(8,128)}) %reduce-scatter.2.cloned.1.call-update) | async-done | bytes 196624 | tf_op jit(solution)/shard_map/reduce_scatter | solution.py:29
  274.1 1.6 broadcast_divide_fusion.1
  (32 shorter events, 2.5 us)
Async XLA Ops:
  7.2 2.1 copy-start
  7.2 160.1 %all-reduce.3.cloned.1.call-start = ((), (), s32[]{:S(2)}) async-start(), calls=%async_computation.1 | async-start | bytes 524288 | tf_op jit(solution)/shard_map/psum | solution.py:25
  9.2 23.0 %copy-start.4 = (bf16[1536,256]{1,0:T(8,128)(2,1)S(1)}, bf16[1536,256]{1,0:T(8,128)(2,1)}, u32[]{:S(2)}) copy-start(bf16[1536,256]{1,0:T(8,128)(2,1)} %param.6) | copy-start | bytes 2359300
  32.2 1.7 copy-start.2
  33.9 29.2 %copy-start.6 = (s32[8]{0:T(128)S(1)}, s32[8]{0:T(128)}, u32[]{:S(2)}) copy-start(s32[8]{0:T(128)} %param.7) | copy-start | bytes 100
  33.9 26.2 %collective-permute-start = (f32[1024,256]{1,0:T(8,128)S(1)}, f32[1024,256]{1,0:T(8,128)S(1)}, u32[]{:S(2)}, u32[]{:S(2)}) collective-permute-start(f32[1024,256]{1,0:T(8,128)S(1)} %convolution_multiply_fusion), channel_id=1, source_target_pairs={{0,1},{1,0},{2,3},{3,2},{4,5},{5,4},{6,7},{7,6},{8,9},{9,8},{10,11... | collective-permute-start | bytes 3145736 | tf_op jit(solution)/shard_map/ppermute | solution.py:21
  60.2 47.8 %collective-permute-start.1 = (f32[1024,256]{1,0:T(8,128)S(1)}, f32[1024,256]{1,0:T(8,128)}, u32[]{:S(2)}, u32[]{:S(2)}) collective-permute-start(f32[1024,256]{1,0:T(8,128)S(1)} %add.37), channel_id=1, source_target_pairs={{0,2},{1,3},{2,0},{3,1},{4,6},{5,7},{6,4},{7,5},{8,10},{9,11},{10,... | collective-permute-start | bytes 3145736 | tf_op jit(solution)/shard_map/ppermute | solution.py:21
  112.2 161.9 %reduce-scatter.2.cloned.1.call-start = ((), (), s32[]{:S(2)}) async-start(), calls=%async_computation.2 | async-start | bytes 1769472 | tf_op jit(solution)/shard_map/reduce_scatter | solution.py:29
  114.7 116.0 %copy-start.1 = (f32[256,1024]{0,1:T(8,128)S(1)}, f32[256,1024]{0,1:T(8,128)}, u32[]{:S(2)}) copy-start(f32[256,1024]{0,1:T(8,128)} %add_bitcast_fusion) | copy-start | bytes 3145732
  209.6 0.7 copy-start.5
  230.7 3.3 %copy-start.3 = (bf16[1024,1536]{1,0:T(8,128)(2,1)S(1)}, bf16[1024,1536]{1,0:T(8,128)(2,1)}, u32[]{:S(2)}) copy-start(bf16[1024,1536]{1,0:T(8,128)(2,1)} %copy-done.2) | copy-start | bytes 9437188
Sparse Core Ops, SparseCore 0:
  112.3 54.8 all-reduce.2
  236.4 37.6 reduce-scatter.1
